TPU v7x, 16 devices: a 4x2x1 block of a 4x4x8 slice. The times are simulated.
16 devices in a mesh: rep: 2 (over y, z), dp: 8 (over x, core).
Axes of the slice: x: 4, y: 2, z: 1, core: 2. Of those that a mesh axis runs over, the one named last changes fastest.
The devices are a block of a 4x4x8 slice.
Arguments:
- g_w_gate: bfloat16 [16, 2, 1024, 4096], P(('rep', 'dp')), parts along dimension 0
- g_w_up: bfloat16 [16, 2, 1024, 4096], P(('rep', 'dp')), parts along dimension 0
- g_w_down: bfloat16 [16, 2, 4096, 1024], P(('rep', 'dp')), parts along dimension 0
- w_gate: bfloat16 [2, 1024, 4096], replicated
- w_up: bfloat16 [2, 1024, 4096], replicated
- w_down: bfloat16 [2, 4096, 1024], replicated
- m_w_gate: float32 [2, 1024, 4096], P(None, 'dp')
- m_w_up: float32 [2, 1024, 4096], P(None, 'dp')
- m_w_down: float32 [2, 4096, 1024], P(None, 'dp')
- v_w_gate: float32 [2, 1024, 4096], P(None, 'dp')
- v_w_up: float32 [2, 1024, 4096], P(None, 'dp')
- v_w_down: float32 [2, 4096, 1024], P(None, 'dp')
Outputs:
- output 1: bfloat16 [4, 1024, 4096], P('rep'), parts along dimension 0
- output 2: bfloat16 [4, 1024, 4096], P('rep'), parts along dimension 0
- output 3: bfloat16 [4, 4096, 1024], P('rep'), parts along dimension 0
- output 4: float32 [4, 1024, 4096], P('rep', 'dp'), parts along dimension 0
- output 5: float32 [4, 1024, 4096], P('rep', 'dp'), parts along dimension 0
- output 6: float32 [4, 4096, 1024], P('rep', 'dp'), parts along dimension 0
- output 7: float32 [4, 1024, 4096], P('rep', 'dp'), parts along dimension 0
- output 8: float32 [4, 1024, 4096], P('rep', 'dp'), parts along dimension 0
- output 9: float32 [4, 4096, 1024], P('rep', 'dp'), parts along dimension 0
There are 2 independent parts. A program takes and returns all parts, laid end to end along the dimension named above; an argument that names none is the same for every part.
All inputs are finite; a program needn't handle non-finite values.
Results may differ from a plain program's by a relative error of at most 0.022.
Values are sent between devices in bfloat16 or wider.
A program may use at most 768 MiB of HBM per device.

v0:
```python
import jax
import jax.numpy as jnp
from jax import lax
from jax.sharding import PartitionSpec as P


def adamw(w, m, v, g):
    m = 0.9 * m + 0.1 * g
    v = 0.95 * v + 0.05 * g * g
    step = m * lax.rsqrt(v + 1e-8) + 0.1 * w
    return (w - 0.02 * step).astype(jnp.bfloat16), m, v


def solution(mesh):
    def step(*arrays):
        terms, weights, m, v = (arrays[i : i + 3] for i in (0, 3, 6, 9))
        gradients = [lax.psum_scatter(t[0], "dp", scatter_dimension=1, tiled=True).astype(jnp.float32) for t in terms]
        me = lax.axis_index("dp")
        own = [lax.dynamic_slice_in_dim(w, me * one.shape[1], one.shape[1], 1).astype(jnp.float32) for w, one in zip(weights, m, strict=True)]
        new = [adamw(w, m, v, g) for w, m, v, g in zip(own, m, v, gradients, strict=True)]
        whole = [lax.all_gather(one[0], "dp", axis=1, tiled=True) for one in new]
        return (*whole, *(one[1] for one in new), *(one[2] for one in new))

    all_of, cut = P(None, None, None), P(None, "dp", None)
    return jax.shard_map(
        step,
        mesh=mesh,
        in_specs=(P(("rep", "dp"), None, None, None),) * 3 + (all_of,) * 3 + (cut,) * 6,
        out_specs=(P("rep", None, None),) * 3 + (P("rep", "dp", None),) * 6,
        check_vma=False,
    )
```

profile of v0, /device:TPU:113, one launch (start us, length us, event | category | flops | bytes accessed | tf_op | source)
XLA Modules:
  0.0 572.1 jit_solution(17951541746850177787)
XLA Ops:
  7.2 0.1 reduce-scatter.8.cloned.1.call-start
  7.3 0.7 reduce-scatter.8.cloned.1.call-update
  8.0 0.1 reduce-scatter.6.cloned.1.call-start
  8.1 0.7 reduce-scatter.6.cloned.1.call-update
  8.8 0.1 reduce-scatter.4.cloned.1.call-start
  8.9 0.7 reduce-scatter.4.cloned.1.call-update
  9.6 0.1 all-gather.8.cloned.1.call-start
  9.7 91.0 %reduce-scatter.8.cloned.1.call-done = bf16[2,512,1024]{2,1,0:T(8,128)(2,1)} async-done(((bf16[2,4096,1024]{2,1,0:T(8,128)(2,1)}), bf16[2,512,1024]{2,1,0:T(8,128)(2,1)}) %reduce-scatter.8.cloned.1.call-update) | async-done | bytes 2097168 | tf_op jit(solution)/shard_map/reduce_scatter | solution.py:17
  100.6 8.1 %fusion.10 = (bf16[2,512,1024]{2,1,0:T(8,128)(2,1)}, f32[2,512,1024]{2,1,0:T(8,128)}, f32[2,512,1024]{2,1,0:T(8,128)}) fusion(bf16[2,4096,1024]{2,1,0:T(8,128)(2,1)} %param.17, s32[]{:T(128)S(6)} %select_n.8, bf16[2,512,1024]{2,1,0:T(8,128)(2,1)} %reduce-scatter.8.cloned.1.call-done, f32[2,512,1024]{2,1,0:T(8,128)} %param.23, f32[2,512,1024]{2,1,0:T(8,128)} %param.20), kind=kLoop, calls=%fused_computation.22 | loop fusion | flops 16777216 | bytes 23068676 | tf_op jit(solution)/shard_map/convert_element_type | solution.py:11
  108.8 0.1 all-gather.8.cloned.1.call-update
  108.8 0.1 all-gather.6.cloned.1.call-start
  108.9 81.5 %reduce-scatter.6.cloned.1.call-done = bf16[2,128,4096]{2,1,0:T(8,128)(2,1)} async-done(((bf16[2,1024,4096]{2,1,0:T(8,128)(2,1)}), bf16[2,128,4096]{2,1,0:T(8,128)(2,1)}) %reduce-scatter.6.cloned.1.call-update) | async-done | bytes 2097168 | tf_op jit(solution)/shard_map/reduce_scatter | solution.py:17
  190.4 8.3 %fusion.6 = (bf16[2,128,4096]{2,1,0:T(8,128)(2,1)}, f32[2,128,4096]{2,1,0:T(8,128)}, f32[2,128,4096]{2,1,0:T(8,128)}) fusion(bf16[2,1024,4096]{2,1,0:T(8,128)(2,1)} %param.16, s32[]{:T(128)S(6)} %select_n.7, bf16[2,128,4096]{2,1,0:T(8,128)(2,1)} %reduce-scatter.6.cloned.1.call-done, f32[2,128,4096]{2,1,0:T(8,128)} %param.22, f32[2,128,4096]{2,1,0:T(8,128)} %param.19), kind=kLoop, calls=%fused_computation.18 | loop fusion | flops 16777216 | bytes 23068676 | tf_op jit(solution)/shard_map/convert_element_type | solution.py:11
  198.8 0.1 all-gather.4.cloned.1.call-start
  198.9 81.3 %reduce-scatter.4.cloned.1.call-done = bf16[2,128,4096]{2,1,0:T(8,128)(2,1)} async-done(((bf16[2,1024,4096]{2,1,0:T(8,128)(2,1)}), bf16[2,128,4096]{2,1,0:T(8,128)(2,1)}) %reduce-scatter.4.cloned.1.call-update) | async-done | bytes 2097168 | tf_op jit(solution)/shard_map/reduce_scatter | solution.py:17
  280.2 8.3 %fusion.2 = (bf16[2,128,4096]{2,1,0:T(8,128)(2,1)}, f32[2,128,4096]{2,1,0:T(8,128)}, f32[2,128,4096]{2,1,0:T(8,128)}) fusion(bf16[2,1024,4096]{2,1,0:T(8,128)(2,1)} %param.15, s32[]{:T(128)S(6)} %select_n.7, bf16[2,128,4096]{2,1,0:T(8,128)(2,1)} %reduce-scatter.4.cloned.1.call-done, f32[2,128,4096]{2,1,0:T(8,128)} %param.21, f32[2,128,4096]{2,1,0:T(8,128)} %param.18), kind=kLoop, calls=%fused_computation.14 | loop fusion | flops 16777216 | bytes 23068676 | tf_op jit(solution)/shard_map/convert_element_type | solution.py:11
  288.6 75.2 %all-gather.8.cloned.1.call-done = bf16[2,4096,1024]{2,1,0:T(8,128)(2,1)} async-done(((bf16[2,512,1024]{2,1,0:T(8,128)(2,1)}), bf16[2,4096,1024]{2,1,0:T(8,128)(2,1)}) %all-gather.8.cloned.1.call-update) | async-done | bytes 16777232 | tf_op jit(solution)/shard_map/all_gather | solution.py:21
  363.9 83.7 %all-gather.6.cloned.1.call-done = bf16[2,1024,4096]{2,1,0:T(8,128)(2,1)} async-done(((bf16[2,128,4096]{2,1,0:T(8,128)(2,1)}), bf16[2,1024,4096]{2,1,0:T(8,128)(2,1)}) %all-gather.6.cloned.1.call-update) | async-done | bytes 16777232 | tf_op jit(solution)/shard_map/all_gather | solution.py:21
  447.5 83.7 %all-gather.4.cloned.1.call-done = bf16[2,1024,4096]{2,1,0:T(8,128)(2,1)} async-done(((bf16[2,128,4096]{2,1,0:T(8,128)(2,1)}), bf16[2,1024,4096]{2,1,0:T(8,128)(2,1)}) %all-gather.4.cloned.1.call-update) | async-done | bytes 16777232 | tf_op jit(solution)/shard_map/all_gather | solution.py:21
  531.2 16.8 %copy.24 = bf16[2,1024,4096]{2,1,0:T(8,128)(2,1)} copy(bf16[2,1024,4096]{2,1,0:T(8,128)(2,1)} %all-gather.4.cloned.1.call-done) | data formatting | bytes 33554432
  548.0 8.5 %copy.25 = bf16[2,1024,4096]{2,1,0:T(8,128)(2,1)} copy(bf16[2,1024,4096]{2,1,0:T(8,128)(2,1)S(1)} %copy-done) | data formatting | bytes 33554432
  556.5 1.4 slice-done.2
  557.9 1.2 slice-done.3
  559.1 6.2 %copy.26 = bf16[2,4096,1024]{2,1,0:T(8,128)(2,1)} copy(bf16[2,4096,1024]{2,1,0:T(8,128)(2,1)S(1)} %bitcast.7) | data formatting | bytes 33554432
  (11 shorter events, 0.1 us)
Async XLA Ops:
  7.2 93.4 %reduce-scatter.8.cloned.1.call-start = ((), (), s32[]{:S(2)}) async-start(), calls=%async_computation.7 | async-start | bytes 18874368 | tf_op jit(solution)/shard_map/reduce_scatter | solution.py:17
  8.0 182.4 %reduce-scatter.6.cloned.1.call-start = ((), (), s32[]{:S(2)}) async-start(), calls=%async_computation.5 | async-start | bytes 18874368 | tf_op jit(solution)/shard_map/reduce_scatter | solution.py:17
  8.8 271.4 %reduce-scatter.4.cloned.1.call-start = ((), (), s32[]{:S(2)}) async-start(), calls=%async_computation.3 | async-start | bytes 18874368 | tf_op jit(solution)/shard_map/reduce_scatter | solution.py:17
  9.6 354.3 %all-gather.8.cloned.1.call-start = ((), (), s32[]{:S(2)}) async-start(), calls=%async_computation.8 | async-start | bytes 18874368 | tf_op jit(solution)/shard_map/all_gather | solution.py:21
  108.8 338.7 %all-gather.6.cloned.1.call-start = ((), (), s32[]{:S(2)}) async-start(), calls=%async_computation.6 | async-start | bytes 18874368 | tf_op jit(solution)/shard_map/all_gather | solution.py:21
  198.8 332.4 %all-gather.4.cloned.1.call-start = ((), (), s32[]{:S(2)}) async-start(), calls=%async_computation.4 | async-start | bytes 18874368 | tf_op jit(solution)/shard_map/all_gather | solution.py:21
  531.2 16.8 %copy-start = (bf16[2,1024,4096]{2,1,0:T(8,128)(2,1)S(1)}, bf16[2,1024,4096]{2,1,0:T(8,128)(2,1)}, u32[]{:S(2)}) copy-start(bf16[2,1024,4096]{2,1,0:T(8,128)(2,1)} %all-gather.6.cloned.1.call-done) | copy-start | bytes 50331652
  531.2 25.3 %slice-start = ((s8[16777216]{0:T(1024)(128)(4,1)}), s8[4194304]{0:T(1024)(128)(4,1)S(1)}, s32[]{:S(2)}) async-start(s8[16777216]{0:T(1024)(128)(4,1)} %bitcast.6), calls=%async_computation.9 | async-start | bytes 8388608
  531.2 25.3 %slice-start.1 = ((s8[16777216]{0:T(1024)(128)(4,1)}), s8[4194304]{0:T(1024)(128)(4,1)S(1)}, s32[]{:S(2)}) async-start(s8[16777216]{0:T(1024)(128)(4,1)} %bitcast.6), calls=%async_computation.10 | async-start | bytes 8388608
  548.0 9.9 %slice-start.2 = ((s8[16777216]{0:T(1024)(128)(4,1)}), s8[4194304]{0:T(1024)(128)(4,1)S(1)}, s32[]{:S(2)}) async-start(s8[16777216]{0:T(1024)(128)(4,1)} %bitcast.6), calls=%async_computation.11 | async-start | bytes 8388608
  548.0 11.1 %slice-start.3 = ((s8[16777216]{0:T(1024)(128)(4,1)}), s8[4194304]{0:T(1024)(128)(4,1)S(1)}, s32[]{:S(2)}) async-start(s8[16777216]{0:T(1024)(128)(4,1)} %bitcast.6), calls=%async_computation.12 | async-start | bytes 8388608
Sparse Core Ops, SparseCore 0:
  10.4 90.1 reduce-scatter.7
  103.0 87.3 reduce-scatter.5
  192.8 87.3 reduce-scatter.3
  282.2 81.5 all-gather.7
  365.9 81.6 all-gather.5
  449.5 81.6 all-gather.3
where the time goes:
time: 572 us
  waiting for transfers between devices  499 us (87%)
  local copies, waits for them, and re-layouts  34.1 us (6%)
  other arithmetic  24.8 us (4%)
  between operations  14.2 us (2%)
    reduce_scatter x3, waiting for transfers between devices, step(): lax.psum_scatter(t[0], 'dp', scatter_dimension=1, tiled=True)  254 us
    all_gather x3, waiting for transfers between devices, step(): whole = [lax.all_gather(one[0], 'dp', axis=1, tiled=True) for one in new]  243 us
    unnamed x13, local copies, waits for them, and re-layouts  34.1 us
    convert_element_type x3, other arithmetic, adamw(): return ((w - 0.02 * step).astype(jnp.bfloat16), m, v)  24.8 us
  transfers between devices with their start and end apart: 6, of which 6 were waited for; matrix products, arithmetic and copies ran while one was open for 4% of the time, Pallas kernels for 0%

commit v1 on v0

v1 whole, which is shorter than its diff:
```python
import functools

import jax
import jax.numpy as jnp
from jax import lax
from jax.experimental import pallas as pl
from jax.experimental.pallas import tpu as pltpu
from jax.sharding import PartitionSpec as P

MESH = pl.DeviceIdType.MESH
ROWS, COLS = 128, 1024
HALF = ROWS // 2
SUB = 16
SLOTS = 4
CORES = 2
A, B = slice(0, HALF), slice(HALF, ROWS)


def adamw(w, m, v, g):
    m = 0.9 * m + 0.1 * g
    v = 0.95 * v + 0.05 * g * g
    step = m * lax.rsqrt(v + 1e-8) + 0.1 * w
    return (w - 0.02 * step).astype(jnp.bfloat16), m, v


def row_loop(first, rows, body):
    def step(i, carry):
        body(pl.ds(pl.multiple_of(first + i * SUB, SUB), SUB))
        return carry

    lax.fori_loop(0, rows // SUB, step, 0)


def kernel(axis, chips, per, units, *refs):
    g, w, m, v = (refs[i : i + 3] for i in (0, 3, 6, 9))
    out, m_out, v_out = (refs[i : i + 3] for i in (12, 15, 18))
    own, pair, arrived, hop, w_v, m_v, v_v = refs[21:28]
    (load_sem, store_sem, pair_sem, hop_sem, arrived_sem, left_sem, right_sem, far_sem, send_sem, gather_sem, tail_sem) = refs[28:]

    me = lax.axis_index(axis)
    chip, core = me // CORES, lax.rem(me, CORES)
    other = 1 - core
    right_chip, left_chip, far_chip = (lax.rem(chip + d, chips) for d in (1, chips - 1, 2))
    right, left, partner = right_chip * CORES + core, left_chip * CORES + core, chip * CORES + other

    def to(device):
        return {"device_id": {axis: device}, "device_id_type": MESH}

    def part(k, u):
        rest = u - k * per
        quarters = per // 2
        return rest // quarters, lax.rem(rest, quarters)

    def block(ref, k, u, who, which):
        layer, q = part(k, u)
        if k < 2:
            return ref.at[layer, who, which, :, pl.ds(pl.multiple_of(q * COLS, COLS), COLS)]
        return ref.at[layer, who, which, q]

    def moment(ref, k, u):
        layer, q = part(k, u)
        if k < 2:
            return ref.at[layer, :, pl.ds(pl.multiple_of(q * COLS, COLS), COLS)]
        return ref.at[layer, q]

    def each_weight(u, body):
        for k in range(3):
            pl.when((u >= k * per) & (u < (k + 1) * per))(functools.partial(body, k))

    def loads(k, u):
        slot = lax.rem(u, SLOTS)
        return (
            pltpu.make_async_copy(block(g[k], k, u, slice(None), core), own.at[slot], load_sem.at[slot, 0]),
            pltpu.make_async_copy(block(w[k], k, u, chip, core), w_v.at[slot], load_sem.at[slot, 1]),
            pltpu.make_async_copy(moment(m[k], k, u), m_v.at[slot], load_sem.at[slot, 2]),
            pltpu.make_async_copy(moment(v[k], k, u), v_v.at[slot], load_sem.at[slot, 3]),
        )

    def stores(k, u):
        slot = lax.rem(u, SLOTS)
        return (
            pltpu.make_async_copy(m_v.at[slot], moment(m_out[k], k, u), store_sem.at[slot, 0]),
            pltpu.make_async_copy(v_v.at[slot], moment(v_out[k], k, u), store_sem.at[slot, 1]),
        )

    def remote(src, dst, send, recv, device):
        return pltpu.make_async_remote_copy(src_ref=src, dst_ref=dst, send_sem=send, recv_sem=recv, **to(device))

    def load(u):
        def body(k):
            for copy in loads(k, u):
                copy.start()
            remote(block(g[k], k, u, slice(None), other), pair.at[u], send_sem.at[k], pair_sem.at[u], partner).start()

        each_weight(u, body)

    def first_hop(u):
        slot = lax.rem(u, SLOTS)
        pltpu.make_async_copy(own.at[slot], own.at[slot], load_sem.at[slot, 0]).wait()
        pltpu.make_async_copy(pair.at[u], pair.at[u], pair_sem.at[u]).wait()

        def add(who, first, rows):
            def body(r):
                pair[u, who, r, :] = (own[slot, who, r, :].astype(jnp.float32) + pair[u, who, r, :].astype(jnp.float32)).astype(jnp.bfloat16)

            row_loop(first, rows, body)

        add(far_chip, 0, ROWS)
        remote(pair.at[u, far_chip, A], hop.at[u, A], send_sem.at[3], hop_sem.at[u], right).start()
        remote(pair.at[u, far_chip, B], hop.at[u, B], send_sem.at[3], hop_sem.at[u], left).start()
        add(right_chip, HALF, HALF)
        remote(pair.at[u, right_chip, B], arrived.at[u, 0, B], send_sem.at[3], arrived_sem.at[u], right).start()
        add(left_chip, 0, HALF)
        remote(pair.at[u, left_chip, A], arrived.at[u, 1, A], send_sem.at[3], arrived_sem.at[u], left).start()

    def second_hop(u):
        slot = lax.rem(u, SLOTS)
        pltpu.make_async_copy(hop.at[u], hop.at[u], hop_sem.at[u]).wait()

        def add(who, first, rows):
            def body(r):
                total = own[slot, who, r, :].astype(jnp.float32) + pair[u, who, r, :].astype(jnp.float32)
                hop[u, r, :] = (total + hop[u, r, :].astype(jnp.float32)).astype(jnp.bfloat16)

            row_loop(first, rows, body)

        add(right_chip, 0, HALF)
        remote(hop.at[u, A], arrived.at[u, 0, A], send_sem.at[4], arrived_sem.at[u], right).start()
        add(left_chip, HALF, HALF)
        remote(hop.at[u, B], arrived.at[u, 1, B], send_sem.at[4], arrived_sem.at[u], left).start()

    def update(u):
        slot = lax.rem(u, SLOTS)
        pltpu.make_async_copy(arrived.at[u], arrived.at[u], arrived_sem.at[u]).wait()
        for i, ref in enumerate((w_v, m_v, v_v)):
            pltpu.make_async_copy(ref.at[slot], ref.at[slot], load_sem.at[slot, 1 + i]).wait()

        def body(r):
            total = own[slot, chip, r, :].astype(jnp.float32) + pair[u, chip, r, :].astype(jnp.float32)
            total = total + arrived[u, 0, r, :].astype(jnp.float32)
            total = total + arrived[u, 1, r, :].astype(jnp.float32)
            total = total.astype(jnp.bfloat16).astype(jnp.float32)
            new_w, new_m, new_v = adamw(w_v[slot, r, :].astype(jnp.float32), m_v[slot, r, :], v_v[slot, r, :], total)
            arrived[u, 0, r, :] = new_w
            m_v[slot, r, :] = new_m
            v_v[slot, r, :] = new_v

        row_loop(0, ROWS, body)

        def send(k):
            new, where = arrived.at[u, 0], block(out[k], k, u, chip, core)
            remote(new, where, send_sem.at[5], left_sem.at[u], right).start()
            remote(new, where, send_sem.at[6], right_sem.at[u], left).start()
            remote(new, where, send_sem.at[7], gather_sem.at[k], partner).start()
            pltpu.make_async_copy(new, where, tail_sem).start()
            for copy in stores(k, u):
                copy.start()

        each_weight(u, send)

    def stored(u):
        def body(k):
            for copy in stores(k, u):
                copy.wait()

        each_weight(u, body)

    def forward(u):
        def body(k):
            from_left, from_right = block(out[k], k, u, left_chip, core), block(out[k], k, u, right_chip, core)
            pltpu.make_async_copy(from_left, from_left, left_sem.at[u]).wait()
            remote(from_left.at[A], from_left.at[A], send_sem.at[8], far_sem.at[u], right).start()
            remote(from_left, from_left, send_sem.at[9], gather_sem.at[k], partner).start()
            pltpu.make_async_copy(from_right, from_right, right_sem.at[u]).wait()
            remote(from_right.at[B], from_right.at[B], send_sem.at[10], far_sem.at[u], left).start()
            remote(from_right, from_right, send_sem.at[11], gather_sem.at[k], partner).start()

        each_weight(u, body)

    def last(u):
        def body(k):
            from_far = block(out[k], k, u, far_chip, core)
            pltpu.make_async_copy(from_far, from_far, far_sem.at[u]).wait()
            remote(from_far, from_far, send_sem.at[12], gather_sem.at[k], partner).start()

        each_weight(u, body)

    barrier = pltpu.get_barrier_semaphore()
    for device in (left, right, partner):
        pl.semaphore_signal(barrier, inc=1, **to(device))
    pl.semaphore_wait(barrier, 3)

    load(0)

    def step(t, carry):
        @pl.when((t >= SLOTS - 1) & (t < units + SLOTS - 1))
        def _():
            stored(t - (SLOTS - 1))

        @pl.when(t < units - 1)
        def _():
            load(t + 1)

        for lag, stage in enumerate((first_hop, second_hop, update, forward, last)):
            pl.when((t >= lag) & (t < units + lag))(functools.partial(stage, t - lag))
        return carry

    lax.fori_loop(0, units + 4, step, 0)

    for k in range(3):
        sent = g[k].at[:, :, other]
        pltpu.make_async_copy(sent, sent, send_sem.at[k]).wait()
    for i, ref in ((3, arrived), (4, hop), (5, hop), (6, hop), (7, hop), (8, hop.at[:, A]), (9, hop), (10, hop.at[:, B]), (11, hop), (12, hop)):
        pltpu.make_async_copy(ref, ref, send_sem.at[i]).wait()
    for k in range(3):
        got = out[k].at[:, :, other]
        pltpu.make_async_copy(got, got, gather_sem.at[k]).wait()
    pltpu.make_async_copy(hop, hop, tail_sem).wait()


def solution(mesh):
    axis = "dp"
    chips = mesh.shape[axis] // CORES
    assert chips == 4

    def step(*arrays):
        def cut(x, rows, columns, split):
            lead = (x.shape[0],) + ((chips, CORES) if split else ())
            return x.reshape(*lead, *((rows, columns) if columns > COLS else (rows // ROWS, ROWS, columns)))

        shapes = [a.shape for a in arrays[6:9]]
        assert all(s[1] == ROWS for s in shapes[:2])
        per = shapes[0][0] * shapes[0][2] // COLS
        units = 3 * per
        g = [cut(a[0], s[1], s[2], True) for a, s in zip(arrays[:3], shapes, strict=True)]
        w = [cut(a, s[1], s[2], True) for a, s in zip(arrays[3:6], shapes, strict=True)]
        moments = [cut(a, s[1], s[2], False) for a, s in zip(arrays[6:], shapes + shapes, strict=True)]
        hbm = pl.BlockSpec(memory_space=pltpu.HBM)
        result = pl.pallas_call(
            functools.partial(kernel, axis, chips, per, units),
            out_shape=[jax.ShapeDtypeStruct(x.shape, x.dtype) for x in (*w, *moments)],
            in_specs=[hbm] * 12,
            out_specs=[hbm] * 9,
            scratch_shapes=[
                pltpu.VMEM((SLOTS, chips, ROWS, COLS), jnp.bfloat16),
                pltpu.VMEM((units, chips, ROWS, COLS), jnp.bfloat16),
                pltpu.VMEM((units, 2, ROWS, COLS), jnp.bfloat16),
                pltpu.VMEM((units, ROWS, COLS), jnp.bfloat16),
                pltpu.VMEM((SLOTS, ROWS, COLS), jnp.bfloat16),
                pltpu.VMEM((SLOTS, ROWS, COLS), jnp.float32),
                pltpu.VMEM((SLOTS, ROWS, COLS), jnp.float32),
                pltpu.SemaphoreType.DMA((SLOTS, 4)),
                pltpu.SemaphoreType.DMA((SLOTS, 2)),
                pltpu.SemaphoreType.DMA((units,)),
                pltpu.SemaphoreType.DMA((units,)),
                pltpu.SemaphoreType.DMA((units,)),
                pltpu.SemaphoreType.DMA((units,)),
                pltpu.SemaphoreType.DMA((units,)),
                pltpu.SemaphoreType.DMA((units,)),
                pltpu.SemaphoreType.DMA((13,)),
                pltpu.SemaphoreType.DMA((3,)),
                pltpu.SemaphoreType.DMA,
            ],
            compiler_params=pltpu.CompilerParams(collective_id=0, has_side_effects=True, vmem_limit_bytes=62 * 1024 * 1024),
        )(*g, *w, *moments)
        return tuple(x.reshape(a.shape) for x, a in zip(result, arrays[3:], strict=True))

    all_of, cut_of = P(None, None, None), P(None, "dp", None)
    return jax.shard_map(
        step,
        mesh=mesh,
        in_specs=(P(("rep", "dp"), None, None, None),) * 3 + (all_of,) * 3 + (cut_of,) * 6,
        out_specs=(P("rep", None, None),) * 3 + (P("rep", "dp", None),) * 6,
        check_vma=False,
    )
```

time: 572 us -> 473 us (0.83)
  waiting for transfers between devices: 499 us -> 0 us
  Pallas kernels: 0 us -> 416 us
  other arithmetic: 24.8 us -> 0.01 us
  local copies, waits for them, and re-layouts: 34.1 us -> 55.5 us
  between operations: 14.2 us -> 0.7 us
    pallas_call x0 -> x1, Pallas kernels: none -> 416 us  [step(): pl.pallas_call(functools.partial(kernel, axis, chips, per, units), out_sh...]
    reduce_scatter x3 -> x0, waiting for transfers between devices: 254 us -> none  [step(): lax.psum_scatter(t[0], 'dp', scatter_dimension=1, tiled=True)]
    all_gather x3 -> x0, waiting for transfers between devices: 243 us -> none  [step(): whole = [lax.all_gather(one[0], 'dp', axis=1, tiled=True) for one in new]]
    convert_element_type x3 -> x0, other arithmetic: 24.8 us -> none  [adamw(): return ((w - 0.02 * step).astype(jnp.bfloat16), m, v)]
    unnamed x13 -> x31, local copies, waits for them, and re-layouts: 34.1 us -> 55.5 us
  transfers between devices with their start and end apart: 6 -> 0, of which waited for: 6 -> 0; matrix products, arithmetic and copies ran while one was open for 4% -> 0% of each run, Pallas kernels for 0% -> 0%
where the time goes in v1:
time: 473 us; the launch traced here: 472 us
  Pallas kernels  416 us (88%)
  local copies, waits for them, and re-layouts  55.5 us (12%)
    pallas_call x1, Pallas kernels, step(): pl.pallas_call(functools.partial(kernel, axis, chips, per, units), out_sh...  416 us
    unnamed x31, local copies, waits for them, and re-layouts  55.5 us

profile of v1, /device:TPU:113, one launch (start us, length us, event | category | flops | bytes accessed | tf_op | source)
XLA Modules:
  0.0 472.3 jit_solution(15566984084458343232)
XLA Ops:
  0.6 416.1 %shard_map.187 = (bf16[2,4,2,128,4096]{4,3,2,1,0:T(8,128)(2,1)}, bf16[2,4,2,128,4096]{4,3,2,1,0:T(8,128)(2,1)}, bf16[2,4,2,4,128,1024]{5,4,3,2,1,0:T(8,128)(2,1)...) custom-call(bf16[2,4,2,128,4096]{4,3,2,1,0:T(8,128)(2,1)} %bitcast.1, ...), custom_call_target="tpu_custom_call" | custom-call | tf_op jit(solution)/shard_map/pallas_call | solution.py:239
  416.8 0.0 copy-start
  416.8 0.0 slice-start
  416.8 0.0 slice-start.1
  416.8 16.8 %copy.30 = bf16[2,1024,4096]{2,1,0:T(8,128)(2,1)} copy(bf16[2,1024,4096]{2,1,0:T(8,128)(2,1)} %bitcast.23) | data formatting | bytes 33554432
  433.6 0.0 copy-done
  433.6 8.5 %copy.31 = bf16[2,1024,4096]{2,1,0:T(8,128)(2,1)} copy(bf16[2,1024,4096]{2,1,0:T(8,128)(2,1)S(1)} %bitcast.22) | data formatting | bytes 33554432
  442.1 0.0 slice-done
  442.1 0.0 slice-done.1
  442.1 1.4 slice-done.2
  443.5 1.2 slice-done.3
  444.7 7.1 %copy.32 = bf16[2,4096,1024]{2,1,0:T(8,128)(2,1)} copy(bf16[2,4096,1024]{2,1,0:T(8,128)(2,1)S(1)} %bitcast.21) | data formatting | bytes 33554432
  451.8 0.0 copy-done.6
  451.8 2.1 copy.33
  453.9 1.6 copy-done.5
  455.5 2.1 copy.34
  457.6 1.6 copy-done.4
  459.2 2.1 copy.35
  461.3 1.6 copy-done.3
  462.9 2.1 copy.36
  465.0 1.6 copy-done.2
  466.6 2.1 copy.37
  468.7 1.6 copy-done.1
  470.3 2.0 copy.38
  (9 shorter events, 0.0 us)
Async XLA Ops:
  416.8 16.8 %copy-start = (bf16[2,4,2,128,4096]{4,3,2,1,0:T(8,128)(2,1)S(1)}, bf16[2,4,2,128,4096]{4,3,2,1,0:T(8,128)(2,1)}, u32[]{:S(2)}) copy-start(bf16[2,4,2,128,4096]{4,3,2,1,0:T(8,128)(2,1)} %get-tuple-element.19) | copy-start | bytes 50331652
  416.8 25.3 %slice-start = ((s8[16777216]{0:T(1024)(128)(4,1)}), s8[4194304]{0:T(1024)(128)(4,1)S(1)}, s32[]{:S(2)}) async-start(s8[16777216]{0:T(1024)(128)(4,1)} %bitcast.19), calls=%async_computation | async-start | bytes 8388608
  416.8 25.3 %slice-start.1 = ((s8[16777216]{0:T(1024)(128)(4,1)}), s8[4194304]{0:T(1024)(128)(4,1)S(1)}, s32[]{:S(2)}) async-start(s8[16777216]{0:T(1024)(128)(4,1)} %bitcast.19), calls=%async_computation.1 | async-start | bytes 8388608
  433.6 9.9 %slice-start.2 = ((s8[16777216]{0:T(1024)(128)(4,1)}), s8[4194304]{0:T(1024)(128)(4,1)S(1)}, s32[]{:S(2)}) async-start(s8[16777216]{0:T(1024)(128)(4,1)} %bitcast.19), calls=%async_computation.2 | async-start | bytes 8388608
  433.6 11.1 %slice-start.3 = ((s8[16777216]{0:T(1024)(128)(4,1)}), s8[4194304]{0:T(1024)(128)(4,1)S(1)}, s32[]{:S(2)}) async-start(s8[16777216]{0:T(1024)(128)(4,1)} %bitcast.19), calls=%async_computation.3 | async-start | bytes 8388608
  444.7 7.1 %copy-start.6 = (f32[2,128,4096]{2,1,0:T(8,128)S(1)}, f32[2,128,4096]{2,1,0:T(8,128)}, u32[]{:S(2)}) copy-start(f32[2,128,4096]{2,1,0:T(8,128)} %get-tuple-element.39) | copy-start | bytes 12582916
  451.8 3.7 copy-start.5
  455.5 3.7 copy-start.4
  459.2 3.7 copy-start.3
  462.9 3.7 copy-start.2
  466.6 3.7 copy-start.1

commit v2 on v1

--- a/solution.py
+++ b/solution.py
@@ -13,6 +13,8 @@
 SUB = 16
 SLOTS = 4
 CORES = 2
+KEPT = 8
+COPY_SLOTS, COPY_AHEAD = 12, 6
 A, B = slice(0, HALF), slice(HALF, ROWS)
 
 
@@ -31,11 +33,12 @@
     lax.fori_loop(0, rows // SUB, step, 0)
 
 
-def kernel(axis, chips, per, units, *refs):
+def kernel(axis, chips, per, units, kept, *refs):
     g, w, m, v = (refs[i : i + 3] for i in (0, 3, 6, 9))
     out, m_out, v_out = (refs[i : i + 3] for i in (12, 15, 18))
-    own, pair, arrived, hop, w_v, m_v, v_v = refs[21:28]
-    (load_sem, store_sem, pair_sem, hop_sem, arrived_sem, left_sem, right_sem, far_sem, send_sem, gather_sem, tail_sem) = refs[28:]
+    to_right, to_left = refs[21:23]
+    own, pair, arrived, hop, w_v, m_v, v_v = refs[23:30]
+    (load_sem, store_sem, pair_sem, hop_sem, arrived_sem, left_sem, right_sem, far_sem, bounce_sem, send_sem, gather_sem, tail_sem) = refs[30:]
 
     me = lax.axis_index(axis)
     chip, core = me // CORES, lax.rem(me, CORES)
@@ -165,23 +168,53 @@
 
         each_weight(u, body)
 
+    def bounces(k, u):
+        slot = lax.rem(u, SLOTS)
+        from_left, from_right = block(out[k], k, u, left_chip, core), block(out[k], k, u, right_chip, core)
+        return (
+            pltpu.make_async_copy(from_left.at[A], arrived.at[u, 1, A], bounce_sem.at[slot, 0]),
+            pltpu.make_async_copy(from_right.at[B], arrived.at[u, 1, B], bounce_sem.at[slot, 1]),
+        )
+
     def forward(u):
         def body(k):
             from_left, from_right = block(out[k], k, u, left_chip, core), block(out[k], k, u, right_chip, core)
             pltpu.make_async_copy(from_left, from_left, left_sem.at[u]).wait()
-            remote(from_left.at[A], from_left.at[A], send_sem.at[8], far_sem.at[u], right).start()
+
+            @pl.when(u < kept)
+            def _():
+                remote(from_left.at[A], from_left.at[A], send_sem.at[8], far_sem.at[u], right).start()
+
             remote(from_left, from_left, send_sem.at[9], gather_sem.at[k], partner).start()
             pltpu.make_async_copy(from_right, from_right, right_sem.at[u]).wait()
-            remote(from_right.at[B], from_right.at[B], send_sem.at[10], far_sem.at[u], left).start()
+
+            @pl.when(u < kept)
+            def _():
+                remote(from_right.at[B], from_right.at[B], send_sem.at[10], far_sem.at[u], left).start()
+
             remote(from_right, from_right, send_sem.at[11], gather_sem.at[k], partner).start()
+
+            @pl.when(u >= kept)
+            def _():
+                for copy in bounces(k, u):
+                    copy.start()
 
         each_weight(u, body)
 
     def last(u):
         def body(k):
-            from_far = block(out[k], k, u, far_chip, core)
-            pltpu.make_async_copy(from_far, from_far, far_sem.at[u]).wait()
-            remote(from_far, from_far, send_sem.at[12], gather_sem.at[k], partner).start()
+            @pl.when(u < kept)
+            def _():
+                from_far = block(out[k], k, u, far_chip, core)
+                pltpu.make_async_copy(from_far, from_far, far_sem.at[u]).wait()
+                remote(from_far, from_far, send_sem.at[12], gather_sem.at[k], partner).start()
+
+            @pl.when(u >= kept)
+            def _():
+                for copy in bounces(k, u):
+                    copy.wait()
+                pltpu.make_async_copy(arrived.at[u, 1, A], to_right.at[u - kept], bounce_sem.at[SLOTS, 0]).start()
+                pltpu.make_async_copy(arrived.at[u, 1, B], to_left.at[u - kept], bounce_sem.at[SLOTS, 1]).start()
 
         each_weight(u, body)
 
@@ -210,12 +243,78 @@
     for k in range(3):
         sent = g[k].at[:, :, other]
         pltpu.make_async_copy(sent, sent, send_sem.at[k]).wait()
-    for i, ref in ((3, arrived), (4, hop), (5, hop), (6, hop), (7, hop), (8, hop.at[:, A]), (9, hop), (10, hop.at[:, B]), (11, hop), (12, hop)):
+    first = pl.ds(0, kept)
+    for i, ref in ((3, arrived), (4, hop), (5, hop), (6, hop), (7, hop), (8, hop.at[first, A]), (9, hop), (10, hop.at[first, B]), (11, hop), (12, hop.at[first])):
         pltpu.make_async_copy(ref, ref, send_sem.at[i]).wait()
     for k in range(3):
-        got = out[k].at[:, :, other]
+        whole = min(max(kept - k * per, 0), per)
+        got = arrived.at[pl.ds(0, (3 * per + whole) // 2)]
         pltpu.make_async_copy(got, got, gather_sem.at[k]).wait()
     pltpu.make_async_copy(hop, hop, tail_sem).wait()
+    for i, ref in enumerate((to_right, to_left)):
+        pltpu.make_async_copy(ref, ref, bounce_sem.at[SLOTS, i]).wait()
+
+
+def copy_kernel(axis, chips, per, kept, *refs):
+    sources, results, buffers, (in_sem, out_sem) = refs[:9], refs[9:18], refs[18:22], refs[22:]
+    far_chip = lax.rem(lax.axis_index(axis) // CORES + 2, chips)
+    layers = sources[0].shape[0]
+    moves = []
+    for i in range(9):
+        src, dst = sources[i], results[i]
+        if i < 3:
+            for layer in range(layers):
+                for who in range(chips - (i * per + layer * per // layers >= kept)):
+                    for which in range(CORES):
+                        at = (layer, lax.rem(far_chip + 1 + who, chips), which)
+                        moves.append((src.at[at], dst.at[at], i // 2))
+        else:
+            for layer in range(layers):
+                for half in range(2):
+                    at = (layer, pl.ds(half * src.shape[1] // 2, src.shape[1] // 2))
+                    moves.append((src.at[at], dst.at[at], 2 + i % 3 // 2))
+    used = [0] * 4
+    copies = []
+    for src, dst, kind in moves:
+        slot = used[kind] % COPY_SLOTS
+        buffer = buffers[kind].at[slot]
+        copies.append((pltpu.make_async_copy(src, buffer, in_sem.at[kind, slot]), pltpu.make_async_copy(buffer, dst, out_sem.at[kind, slot]), used[kind]))
+        used[kind] += 1
+    kinds = [kind for _, _, kind in moves]
+    waited = set()
+
+    def wait_for(i):
+        if i not in waited:
+            waited.add(i)
+            copies[i][1].wait()
+
+    for i in range(len(copies) + COPY_AHEAD):
+        if i < len(copies):
+            if copies[i][2] >= COPY_SLOTS:
+                wait_for(next(j for j in range(i) if kinds[j] == kinds[i] and copies[j][2] == copies[i][2] - COPY_SLOTS))
+            copies[i][0].start()
+        if i >= COPY_AHEAD:
+            copies[i - COPY_AHEAD][0].wait()
+            copies[i - COPY_AHEAD][1].start()
+    for i in range(len(copies)):
+        wait_for(i)
+
+
+def place_kernel(axis, chips, per, kept, partner, first, second, *refs):
+    results, sem = refs[3:6], refs[6]
+    me = lax.axis_index(axis)
+    far_chip, core = lax.rem(me // CORES + 2, chips), lax.rem(me, CORES)
+    which = 1 - core if partner else core
+    quarters = per // 2
+    for j in range(first.shape[0]):
+        k, rest = (kept + j) // per, (kept + j) % per
+        layer, q = rest // quarters, rest % quarters
+        whole = results[k].at[layer, far_chip, which]
+        where = whole.at[:, pl.ds(q * COLS, COLS)] if k < 2 else whole.at[q]
+        pltpu.make_async_copy(first.at[j], where.at[A], sem.at[0]).start()
+        pltpu.make_async_copy(second.at[j], where.at[B], sem.at[1]).start()
+    pltpu.make_async_copy(first, first, sem.at[0]).wait()
+    pltpu.make_async_copy(second, second, sem.at[1]).wait()
 
 
 def solution(mesh):
@@ -235,12 +334,14 @@
         g = [cut(a[0], s[1], s[2], True) for a, s in zip(arrays[:3], shapes, strict=True)]
         w = [cut(a, s[1], s[2], True) for a, s in zip(arrays[3:6], shapes, strict=True)]
         moments = [cut(a, s[1], s[2], False) for a, s in zip(arrays[6:], shapes + shapes, strict=True)]
-        hbm = pl.BlockSpec(memory_space=pltpu.HBM)
-        result = pl.pallas_call(
-            functools.partial(kernel, axis, chips, per, units),
-            out_shape=[jax.ShapeDtypeStruct(x.shape, x.dtype) for x in (*w, *moments)],
+        hbm, vmem = pl.BlockSpec(memory_space=pltpu.HBM), pl.BlockSpec(memory_space=pltpu.VMEM)
+        results = [jax.ShapeDtypeStruct(x.shape, x.dtype) for x in (*w, *moments)]
+        halves = jax.ShapeDtypeStruct((units - KEPT, HALF, COLS), jnp.bfloat16)
+        *made, to_right, to_left = pl.pallas_call(
+            functools.partial(kernel, axis, chips, per, units, KEPT),
+            out_shape=[*results, halves, halves],
             in_specs=[hbm] * 12,
-            out_specs=[hbm] * 9,
+            out_specs=[hbm] * 11,
             scratch_shapes=[
                 pltpu.VMEM((SLOTS, chips, ROWS, COLS), jnp.bfloat16),
                 pltpu.VMEM((units, chips, ROWS, COLS), jnp.bfloat16),
@@ -257,12 +358,52 @@
                 pltpu.SemaphoreType.DMA((units,)),
                 pltpu.SemaphoreType.DMA((units,)),
                 pltpu.SemaphoreType.DMA((units,)),
+                pltpu.SemaphoreType.DMA((SLOTS + 1, 2)),
                 pltpu.SemaphoreType.DMA((13,)),
                 pltpu.SemaphoreType.DMA((3,)),
                 pltpu.SemaphoreType.DMA,
             ],
             compiler_params=pltpu.CompilerParams(collective_id=0, has_side_effects=True, vmem_limit_bytes=62 * 1024 * 1024),
         )(*g, *w, *moments)
+
+        n = chips * CORES
+        from_left = lax.ppermute(to_right, axis, [(i, (i + CORES) % n) for i in range(n)])
+        from_right = lax.ppermute(to_left, axis, [(i, (i - CORES) % n) for i in range(n)])
+        swap = [(i, i // CORES * CORES + 1 - i % CORES) for i in range(n)]
+        result = pl.pallas_call(
+            functools.partial(copy_kernel, axis, chips, per, KEPT),
+            out_shape=results,
+            in_specs=[hbm] * 9,
+            out_specs=[hbm] * 9,
+            scratch_shapes=[
+                pltpu.VMEM((COPY_SLOTS, ROWS, 4 * COLS), jnp.bfloat16),
+                pltpu.VMEM((COPY_SLOTS, 4, ROWS, COLS), jnp.bfloat16),
+                pltpu.VMEM((COPY_SLOTS, HALF, 4 * COLS), jnp.float32),
+                pltpu.VMEM((COPY_SLOTS, 2, ROWS, COLS), jnp.float32),
+                pltpu.SemaphoreType.DMA((4, COPY_SLOTS)),
+                pltpu.SemaphoreType.DMA((4, COPY_SLOTS)),
+            ],
+            compiler_params=pltpu.CompilerParams(has_side_effects=True, vmem_limit_bytes=52 * 1024 * 1024),
+            cost_estimate=pl.CostEstimate(flops=10**9, bytes_accessed=2**27, transcendentals=0),
+        )(*made)
+
+        def place(result, first, second, partner):
+            new = pl.pallas_call(
+                functools.partial(place_kernel, axis, chips, per, KEPT, partner),
+                out_shape=results[:3],
+                in_specs=[vmem] * 2 + [hbm] * 3,
+                out_specs=[hbm] * 3,
+                input_output_aliases={2: 0, 3: 1, 4: 2},
+                scratch_shapes=[pltpu.SemaphoreType.DMA((2,))],
+                compiler_params=pltpu.CompilerParams(has_side_effects=True, vmem_limit_bytes=16 * 1024 * 1024),
+                cost_estimate=pl.CostEstimate(flops=10**7, bytes_accessed=2**22, transcendentals=0),
+            )(first, second, *result[:3])
+            return [*new, *result[3:]]
+
+        from_left, from_right, *result = lax.optimization_barrier((from_left, from_right, *result))
+        others = lax.ppermute(from_left, axis, swap), lax.ppermute(from_right, axis, swap)
+        result = place(result, from_left, from_right, False)
+        result = place(result, *others, True)
         return tuple(x.reshape(a.shape) for x, a in zip(result, arrays[3:], strict=True))
 
     all_of, cut_of = P(None, None, None), P(None, "dp", None)

time: 473 us -> 431 us (0.911)
  local copies, waits for them, and re-layouts: 55.5 us -> 0 us
  waiting for transfers between devices: 0 us -> 6.63 us
    unnamed x31 -> x0, local copies, waits for them, and re-layouts: 55.5 us -> none
    ppermute x0 -> x4, waiting for transfers between devices: none -> 6.63 us  [the longest x1 3 us: step(): lax.ppermute(from_right, axis, swap)]
    pallas_call x1 -> x4, Pallas kernels: 416 us -> 419 us  [the longest x1 372 us: step(): pl.pallas_call(functools.partial(kernel, axis, chips, per, units, KEPT),...]
  transfers between devices with their start and end apart: 0 -> 4, of which waited for: 0 -> 3; matrix products, arithmetic and copies ran while one was open for 0% -> 0% of each run, Pallas kernels for 0% -> 11%
where the time goes in v2:
time: 431 us
  Pallas kernels  419 us (97%)
  waiting for transfers between devices  6.63 us (2%)
    pallas_call x1, Pallas kernels, step(): pl.pallas_call(functools.partial(kernel, axis, chips, per, units, KEPT),...  372 us
    pallas_call x1, Pallas kernels, step(): pl.pallas_call(functools.partial(copy_kernel, axis, chips, per, KEPT), ou...  43.6 us
  transfers between devices with their start and end apart: 4, of which 3 were waited for; matrix products, arithmetic and copies ran while one was open for 0% of the time, Pallas kernels for 11%

profile of v2, /device:TPU:113, one launch (start us, length us, event | category | flops | bytes accessed | tf_op | source)
XLA Modules:
  0.0 430.5 jit_solution(15772939432196013758)
XLA Ops:
  0.6 371.7 %shard_map.187 = (bf16[2,4,2,128,4096]{4,3,2,1,0:T(8,128)(2,1)}, bf16[2,4,2,128,4096]{4,3,2,1,0:T(8,128)(2,1)}, bf16[2,4,2,4,128,1024]{5,4,3,2,1,0:T(8,128)(2,1)...) custom-call(bf16[2,4,2,128,4096]{4,3,2,1,0:T(8,128)(2,1)} %bitcast.1, ...), custom_call_target="tpu_custom_call" | custom-call | tf_op jit(solution)/shard_map/pallas_call | solution.py:340
  372.4 0.8 collective-permute-start
  373.2 2.0 collective-permute-start.1
  375.2 43.6 %shard_map.188 = (bf16[2,4,2,128,4096]{4,3,2,1,0:T(8,128)(2,1)}, bf16[2,4,2,128,4096]{4,3,2,1,0:T(8,128)(2,1)}, bf16[2,4,2,4,128,1024]{5,4,3,2,1,0:T(8,128)(2,1)...) custom-call(bf16[2,4,2,128,4096]{4,3,2,1,0:T(8,128)(2,1)} %get-tuple, ...), custom_call_target="tpu_custom_call" | custom-call | flops 1000000000 | bytes 134217728 | tf_op jit(solution)/shard_map/pallas_call | solution.py:373
  418.7 1.8 collective-permute-done.first
  420.6 0.0 collective-permute-done.1.second
  420.6 1.2 collective-permute-start.2
  421.7 0.0 collective-permute-start.3
  421.7 2.0 shard_map.189
  423.7 1.8 collective-permute-done.2.first
  425.5 3.0 collective-permute-done.3.second
  428.5 2.0 shard_map.190
Async XLA Ops:
  372.4 48.2 %collective-permute-start = (bf16[16,64,1024]{2,1,0:T(8,128)(2,1)}, bf16[16,64,1024]{2,1,0:T(8,128)(2,1)S(1)}, u32[]{:S(2)}, u32[]{:S(2)}) collective-permute-start(bf16[16,64,1024]{2,1,0:T(8,128)(2,1)} %get-tuple-element.46), channel_id=1, source_target_pairs={{0,2},{1,3},{2,4},{3,5},{4,6},{5,7},{6,0},{7,1},{8,10},{9,11},{10,... | collective-permute-start | bytes 6291464 | tf_op jit(solution)/shard_map/ppermute | solution.py:370
  373.2 47.4 %collective-permute-start.1 = (bf16[16,64,1024]{2,1,0:T(8,128)(2,1)}, bf16[16,64,1024]{2,1,0:T(8,128)(2,1)S(1)}, u32[]{:S(2)}, u32[]{:S(2)}) collective-permute-start(bf16[16,64,1024]{2,1,0:T(8,128)(2,1)} %get-tuple-element.47), channel_id=1, source_target_pairs={{0,6},{1,7},{2,0},{3,1},{4,2},{5,3},{6,4},{7,5},{8,14},{9,15},{10,... | collective-permute-start | bytes 6291464 | tf_op jit(solution)/shard_map/ppermute | solution.py:371
  420.6 4.9 %collective-permute-start.2 = (bf16[16,64,1024]{2,1,0:T(8,128)(2,1)S(1)}, bf16[16,64,1024]{2,1,0:T(8,128)(2,1)S(1)}, u32[]{:S(2)}, u32[]{:S(2)}) collective-permute-start(bf16[16,64,1024]{2,1,0:T(8,128)(2,1)S(1)} %collective-permute-done.first), channel_id=1, source_target_pairs={{0,1},{1,0},{2,3},{3,2},{4,5},{5,4},{6,7},{7,6},{8,9},{9,8},{10,11... | collective-permute-start | bytes 6291464 | tf_op jit(solution)/shard_map/ppermute | solution.py:404
  421.7 6.8 %collective-permute-start.3 = (bf16[16,64,1024]{2,1,0:T(8,128)(2,1)S(1)}, bf16[16,64,1024]{2,1,0:T(8,128)(2,1)S(1)}, u32[]{:S(2)}, u32[]{:S(2)}) collective-permute-start(bf16[16,64,1024]{2,1,0:T(8,128)(2,1)S(1)} %collective-permute-done.1.second), channel_id=1, source_target_pairs={{0,1},{1,0},{2,3},{3,2},{4,5},{5,4},{6,7},{7,6},{8,9},{9,8},{10,11... | collective-permute-start | bytes 6291464 | tf_op jit(solution)/shard_map/ppermute | solution.py:404
